TPU v7x, 512 devices: a whole 4x8x8 slice. The times are simulated.
512 devices in a mesh: row: 32 (over z, x_lo, core), col: 16 (over y, x_hi).
Axes of the slice: x: 4 (x_hi: 2, x_lo: 2; x = x_hi * 2 + x_lo), y: 8, z: 8, core: 2. Of those that a mesh axis runs over, the one named last changes fastest.
Arguments:
- substrate: float32 [4096, 4096], P('row', 'col'), may hold values from 0.05 to 0.95
- activator: float32 [4096, 4096], P('row', 'col'), may hold values from 0 to 0.45
Outputs:
- substrate_section: float32 [4096, 4096], P('row', 'col')
- activator_section: float32 [4096, 4096], P('row', 'col')
All inputs are finite; a program needn't handle non-finite values.
Results may differ from a plain program's by a relative error of at most 0.00023.
Values sent between devices are 32-bit elements; how exact they have to be, the bound alone decides.
No kernel may reach another device: no remote copies, remote signals or barrier semaphores. Data moves between devices by JAX's collectives and lax.ppermute only.
A program may use at most 64 MiB of HBM per device.

v0:
```python
import math
import jax
import jax.numpy as jnp
from jax import lax
from jax.sharding import Mesh
from jax.sharding import PartitionSpec as P

ROW = ("row_0", "row_1", "row_2")
FEED_RATE = 0.037
KILL_RATE = 0.06
TIME_STEP = 8.0
SUBSTRATE_DIFFUSION = 4e-07
ACTIVATOR_DIFFUSION = 2e-07


def split_up(shard, dim, size):
    before, after = (shard.shape[:dim], shard.shape[dim + 1 :])
    return jnp.moveaxis(shard.reshape(*before, size, -1, *after), dim, 0)


def in_order(pieces, dim):
    pieces = jnp.moveaxis(pieces, 0, dim)
    shape = pieces.shape
    return pieces.reshape(*shape[:dim], shape[dim] * shape[dim + 1], *shape[dim + 2 :])


def moved_by_axis(pieces, axes, turns):
    shape = [lax.axis_size(a) for a in axes]
    pieces = pieces.reshape(*shape, *pieces.shape[1:])
    for k in turns:
        pieces = lax.all_to_all(pieces, axes[k], split_axis=k, concat_axis=k, tiled=True)
    return pieces.reshape(-1, *pieces.shape[len(axes) :])


def exchange_by_chip(shard, groups, turns, split_dim, concat_dim):
    size = lax.axis_size(groups[0]) * lax.axis_size(groups[1])
    pieces = split_up(shard, split_dim, size)
    return in_order(moved_by_axis(pieces, groups, turns), concat_dim)


def rotation(left_index, right_index, period, direction):
    phase_index = left_index * right_index % period
    angles = phase_index.astype(jnp.float32) * (2.0 * math.pi / period)
    return (jnp.cos(angles), direction * jnp.sin(angles))


def complex_matrix(size_count, direction):
    indices = jnp.arange(size_count, dtype=jnp.int32)
    cosine_part, sine_part = rotation(indices[:, None], indices[None, :], size_count, direction)
    return jnp.stack([jnp.stack([cosine_part, -sine_part]), jnp.stack([sine_part, cosine_part])])


def transform_last(values, direction):
    part_count, species, middle, length = values.shape
    leading = 64
    second = length // leading
    shaped = values.reshape(part_count, species, middle, leading, second)
    first_matrix = complex_matrix(leading, direction)
    first_pass = jnp.einsum(
        "pqka,qsmab->psmkb", first_matrix, shaped, precision=lax.Precision.HIGHEST
    )
    cosine_part, sine_part = rotation(
        jnp.arange(leading, dtype=jnp.int32)[:, None],
        jnp.arange(second, dtype=jnp.int32)[None, :],
        length,
        direction,
    )
    turned = jnp.stack(
        [
            first_pass[0] * cosine_part - first_pass[1] * sine_part,
            first_pass[0] * sine_part + first_pass[1] * cosine_part,
        ]
    )
    second_matrix = complex_matrix(second, direction)
    second_pass = jnp.einsum(
        "pqkb,qsmjb->psmkj", second_matrix, turned, precision=lax.Precision.HIGHEST
    )
    return second_pass.reshape(part_count, species, middle, length)


def signed_squares(wave_index, total):
    signed = jnp.where(2 * wave_index < total, wave_index, wave_index - total).astype(jnp.float32)
    angular = 2.0 * math.pi * signed
    return angular * angular


def section_factors(row_wave, col_wave, total_rows, total_cols):
    wave_number = signed_squares(row_wave, total_rows) + signed_squares(col_wave, total_cols)
    normalize = 1.0 / (total_rows * total_cols)
    growths = []
    forcings = []
    for diffusion, decay_rate in (
        (SUBSTRATE_DIFFUSION, FEED_RATE),
        (ACTIVATOR_DIFFUSION, FEED_RATE + KILL_RATE),
    ):
        linear = -diffusion * wave_number - decay_rate
        exponent = linear * (0.5 * TIME_STEP)
        growths.append(jnp.exp(exponent) * normalize)
        forcings.append(jnp.expm1(exponent) / linear * normalize)
    return (jnp.stack(growths), jnp.stack(forcings))


def advance(spectra, growth, forcing):
    real_part = spectra[0]
    imag_part = spectra[1]
    return jnp.stack(
        [growth * real_part + forcing * imag_part, growth * imag_part - forcing * real_part]
    )


def col_forward(values):
    return lax.all_to_all(values, "col", split_axis=2, concat_axis=3, tiled=True)


def col_backward(values):
    return lax.all_to_all(values, "col", split_axis=3, concat_axis=2, tiled=True)


def row_forward(values):
    return lax.all_to_all(values, ROW, split_axis=2, concat_axis=3, tiled=True)


def row_backward(values):
    return exchange_by_chip(values, (("row_0", "row_1"), "row_2"), (1, 0), 3, 2)


def on_device(substrate, activator):
    row_count, col_count = substrate.shape
    total_rows = row_count * lax.axis_size(ROW)
    total_cols = col_count * lax.axis_size("col")
    row_index = lax.axis_index(ROW)
    col_index = lax.axis_index("col")
    reaction = substrate * activator * activator
    fields = jnp.stack(
        [jnp.stack([substrate, activator]), jnp.stack([FEED_RATE - reaction, reaction])]
    )
    spectra = transform_last(col_forward(fields), -1)
    spectra = row_forward(col_forward(jnp.swapaxes(spectra, 2, 3)))
    spectra = transform_last(spectra, -1)
    local_cols = col_count // lax.axis_size(ROW)
    col_wave = (
        col_count * col_index
        + local_cols * row_index
        + jnp.arange(local_cols, dtype=jnp.int32)[:, None]
    )
    row_wave = jnp.arange(total_rows, dtype=jnp.int32)[None, :]
    growth, forcing = section_factors(row_wave, col_wave, total_rows, total_cols)
    spectra = transform_last(advance(spectra, growth, forcing), 1)
    spectra = col_backward(row_backward(spectra))
    spectra = jnp.swapaxes(spectra, 2, 3)
    spectra = transform_last(spectra, 1)
    fields = lax.all_to_all(spectra[:1], "col", split_axis=3, concat_axis=2, tiled=True)
    return (fields[0, 0], fields[0, 1])


def solution(mesh):
    split = Mesh(
        mesh.devices.reshape(8, 2, 2, mesh.shape["col"]), ("row_0", "row_1", "row_2", "col")
    )
    placed = (P(ROW, "col"), P(ROW, "col"))
    return jax.shard_map(
        on_device,
        mesh=split,
        in_specs=placed,
        out_specs=(P(ROW, "col"), P(ROW, "col")),
        check_vma=False,
    )
```

profile of v0, /device:TPU:128, one launch (start us, length us, event | category | flops | bytes accessed | tf_op | source)
XLA Modules:
  0.0 240.7 jit_solution(18441862085176898476)
XLA Ops:
  0.6 1.0 stack.54
  1.6 1.0 stack.53
  2.6 1.0 subtract_bitcast_fusion
  4.4 1.0 pad_maximum_fusion.1
  5.4 9.7 %all-to-all-start = ((f32[2,2,128,256]{3,1,0,2:T(2,128)}), f32[2,2,128,256]{3,1,0,2:T(2,128)S(1)}, u32[]{:S(2)}, u32[]{:S(2)}) async-start(f32[2,2,128,256]{3,1,0,2:T(2,128)} %pad_maximum_fusion.1), calls=%async_computation | async-start | bytes 1048576 | tf_op jit(solution)/shard_map/all_to_all | solution.py:112
  15.7 18.2 %all-to-all-done = f32[2,2,128,256]{3,1,0,2:T(2,128)S(1)} async-done(((f32[2,2,128,256]{3,1,0,2:T(2,128)}), f32[2,2,128,256]{3,1,0,2:T(2,128)S(1)}, u32[]{:S(2)}, u32[]{:S(2)}) %all-to-all-start) | async-done | bytes 524320 | tf_op jit(solution)/shard_map/all_to_all | solution.py:112
  34.4 1.8 convolution_bitcast_fusion.7
  36.4 1.8 convolution_bitcast_fusion.6
  38.9 8.2 %copy.66 = f32[2,2,4096,8]{3,1,0,2:T(2,128)} copy(f32[2,2,4096,8]{2,3,1,0:T(8,128)S(1)} %bitcast.164) | data formatting | bytes 1048576 | tf_op jit(solution)/shard_map/transpose | solution.py:138
  47.1 14.9 %reshape.444 = f32[16,1,8192]{2,1,0:T(1,128)S(1)} reshape(f32[4096,2,2,8]{3,2,1,0:T(2,128)} %bitcast.160) | data formatting | bytes 1048576
  62.0 22.1 %all_to_all.94 = f32[16,1,8192]{2,1,0:T(1,128)S(1)} all-to-all(f32[16,1,8192]{2,1,0:T(1,128)S(1)} %reshape.444), channel_id=1, replica_groups=mesh['row_0'=8,'row_1'=2,'row_2'=2,'col'=16] {'col'}, dimensions={0} | all-to-all | bytes 1048576 | tf_op jit(solution)/shard_map/all_to_all | solution.py:112
  84.6 1.9 reduce
  86.5 14.7 %reshape.445 = f32[4096,2,2,8]{3,2,1,0:T(2,128)} reshape(f32[16,8192]{1,0:T(8,128)S(1)} %reduce) | data formatting | bytes 1048576
  101.2 9.5 %copy.67 = f32[2,2,4096,8]{2,3,1,0:T(8,128)S(1)} copy(f32[2,2,4096,8]{3,1,0,2:T(2,128)} %bitcast.161) | data formatting | bytes 1048576 | tf_op jit(solution)/shard_map/all_to_all | solution.py:112
  110.7 1.0 copy.68
  111.7 9.2 %all-to-all-start.2 = ((f32[2,2,256,128]{3,1,0,2:T(2,128)}), f32[2,2,256,128]{3,1,0,2:T(2,128)S(1)}, u32[]{:S(2)}, u32[]{:S(2)}) async-start(f32[2,2,256,128]{3,1,0,2:T(2,128)} %copy.68), calls=%async_computation.2 | async-start | bytes 1048576 | tf_op jit(solution)/shard_map/all_to_all | solution.py:120
  121.5 15.2 %all-to-all-done.2 = f32[2,2,256,128]{3,1,0,2:T(2,128)S(1)} async-done(((f32[2,2,256,128]{3,1,0,2:T(2,128)}), f32[2,2,256,128]{3,1,0,2:T(2,128)S(1)}, u32[]{:S(2)}, u32[]{:S(2)}) %all-to-all-start.2) | async-done | bytes 524320 | tf_op jit(solution)/shard_map/all_to_all | solution.py:120
  137.1 1.8 convolution_bitcast_fusion.5
  139.1 1.8 convolution_bitcast_fusion.4
  141.2 1.0 convolution_bitcast_fusion.3
  142.4 1.8 convolution_bitcast_fusion.2
  144.8 4.2 %all_to_all.95 = f32[16,2,2,2,8,128]{5,0,4,3,2,1:T(8,128)S(1)} all-to-all(f32[16,2,2,2,8,128]{5,0,4,3,2,1:T(8,128)S(1)} %copy.75), channel_id=1, replica_groups=mesh['row_0'=8,'row_1'=2,'row_2'=2,'col'=16] {'row_2'}, dimensions={1} | all-to-all | bytes 1048576 | tf_op jit(solution)/shard_map/all_to_all | solution.py:31
  149.4 20.6 %all_to_all.96 = f32[16,2,2,2,8,128]{5,1,4,3,2,0:T(2,128)S(1)} all-to-all(f32[16,2,2,2,8,128]{5,1,4,3,2,0:T(2,128)S(1)} %copy.76), channel_id=1, replica_groups=mesh['row_0'=8,'row_1'=2,'row_2'=2,'col'=16] {'row_0','row_1'}, dimensions={0} | all-to-all | bytes 1048576 | tf_op jit(solution)/shard_map/all_to_all | solution.py:31
  170.3 21.7 %all_to_all.97 = f32[2,2,256,128]{2,1,0,3:T(2,128)S(1)} all-to-all(f32[2,2,256,128]{2,1,0,3:T(2,128)S(1)} %copy.78), channel_id=1, replica_groups=mesh['row_0'=8,'row_1'=2,'row_2'=2,'col'=16] {'col'}, dimensions={3} | all-to-all | bytes 1048576 | tf_op jit(solution)/shard_map/all_to_all | solution.py:116
  192.5 1.8 convolution_bitcast_fusion.1
  194.5 1.8 convolution_bitcast_fusion
  196.4 4.8 %copy.117 = f32[1,2,8,64,64]{2,1,4,3,0:T(2,128)} copy(f32[1,2,8,64,64]{3,4,0,2,1:T(8,128)S(1)} %slice.76) | data formatting | bytes 524288 | tf_op jit(solution)/shard_map/slice | solution.py:152
  201.1 8.3 %reshape.446 = f32[16,1,4096]{2,1,0:T(1,128)S(1)} reshape(f32[4096,1,2,8]{3,2,1,0:T(2,128)} %bitcast.162) | data formatting | bytes 524288
  209.4 16.5 %all_to_all.98 = f32[16,1,4096]{2,1,0:T(1,128)S(1)} all-to-all(f32[16,1,4096]{2,1,0:T(1,128)S(1)} %reshape.446), channel_id=1, replica_groups=mesh['row_0'=8,'row_1'=2,'row_2'=2,'col'=16] {'col'}, dimensions={0} | all-to-all | bytes 524288 | tf_op jit(solution)/shard_map/all_to_all | solution.py:152
  225.9 1.3 reduce.1
  227.1 7.7 %reshape.447 = f32[4096,1,2,8]{3,2,1,0:T(2,128)} reshape(f32[16,4096]{1,0:T(8,128)S(1)} %reduce.1) | data formatting | bytes 524288
  234.8 5.1 %copy.84 = f32[1,2,16,8,256]{4,3,2,1,0:T(8,128)S(1)} copy(f32[1,2,16,8,256]{3,1,4,2,0:T(2,128)} %bitcast.163) | data formatting | bytes 524288 | tf_op jit(solution)/shard_map/all_to_all | solution.py:152
  (35 shorter events, 7.3 us)
Async XLA Ops:
  5.4 28.5 %all-to-all-start = ((f32[2,2,128,256]{3,1,0,2:T(2,128)}), f32[2,2,128,256]{3,1,0,2:T(2,128)S(1)}, u32[]{:S(2)}, u32[]{:S(2)}) async-start(f32[2,2,128,256]{3,1,0,2:T(2,128)} %pad_maximum_fusion.1), calls=%async_computation | async-start | bytes 1048576 | tf_op jit(solution)/shard_map/all_to_all | solution.py:112
  111.7 25.0 %all-to-all-start.2 = ((f32[2,2,256,128]{3,1,0,2:T(2,128)}), f32[2,2,256,128]{3,1,0,2:T(2,128)S(1)}, u32[]{:S(2)}, u32[]{:S(2)}) async-start(f32[2,2,256,128]{3,1,0,2:T(2,128)} %copy.68), calls=%async_computation.2 | async-start | bytes 1048576 | tf_op jit(solution)/shard_map/all_to_all | solution.py:120
where the time goes:
time: 241 us
  blocking collectives  85 us (35%)
  local copies, waits for them, and re-layouts  81 us (34%)
  waiting for transfers between devices  33.4 us (14%)
  starting transfers between devices  18.9 us (8%)
  matrix products  13.7 us (6%)
  other arithmetic  7.65 us (3%)
    unnamed x4, local copies, waits for them, and re-layouts  45.6 us
    all_to_all x2, blocking collectives, moved_by_axis(): lax.all_to_all(pieces, axes[k], split_axis=k, concat_axis=k, tiled=True)  24.8 us
    all_to_all x1, blocking collectives, col_forward(): lax.all_to_all(values, 'col', split_axis=2, concat_axis=3, tiled=True)  22.1 us
    all_to_all x1, blocking collectives, col_backward(): lax.all_to_all(values, 'col', split_axis=3, concat_axis=2, tiled=True)  21.7 us
    all_to_all x1, waiting for transfers between devices, col_forward(): lax.all_to_all(values, 'col', split_axis=2, concat_axis=3, tiled=True)  18.2 us
    all_to_all x1, blocking collectives, on_device(): lax.all_to_all(spectra[:1], 'col', split_axis=3, concat_axis=2, tiled=True)  16.5 us
    all_to_all x1, waiting for transfers between devices, row_forward(): return lax.all_to_all(values, ROW, split_axis=2, concat_axis=3, tiled=True)  15.2 us
    all_to_all x4, local copies, waits for them, and re-layouts, col_forward(): lax.all_to_all(values, 'col', split_axis=2, concat_axis=3, tiled=True)  11.3 us
  transfers between devices with their start and end apart: 2, of which 2 were waited for; matrix products, arithmetic and copies ran while one was open for 0% of the time, Pallas kernels for 0%

commit v1 on v0

--- a/solution.py
+++ b/solution.py
@@ -149,7 +149,12 @@
     spectra = col_backward(row_backward(spectra))
     spectra = jnp.swapaxes(spectra, 2, 3)
     spectra = transform_last(spectra, 1)
-    fields = lax.all_to_all(spectra[:1], "col", split_axis=3, concat_axis=2, tiled=True)
+    fields = jnp.concatenate(
+        lax.all_to_all(
+            jnp.stack(jnp.split(spectra[:1], lax.axis_size("col"), axis=3)), "col", 0, 0
+        ),
+        axis=2,
+    )
     return (fields[0, 0], fields[0, 1])
 
 

time: 241 us -> 215 us (0.89)
  local copies, waits for them, and re-layouts: 81 us -> 55.6 us
    unnamed x4 -> x17, local copies, waits for them, and re-layouts: 45.6 us -> 29.7 us
    all_to_all x1 -> x0, local copies, waits for them, and re-layouts: 5.12 us -> none  [on_device(): lax.all_to_all(spectra[:1], 'col', split_axis=3, concat_axis=2, tiled=True)]
    slice x2 -> x3, local copies, waits for them, and re-layouts: 4.8 us -> 0.42 us  [on_device(): spectra[:1]]
  transfers between devices with their start and end apart: 2 -> 2, of which waited for: 2 -> 2; matrix products, arithmetic and copies ran while one was open for 0% -> 1% of each run, Pallas kernels for 0% -> 0%
where the time goes in v1:
time: 215 us; the launch traced here: 214 us
  blocking collectives  85 us (40%)
  local copies, waits for them, and re-layouts  55.6 us (26%)
  waiting for transfers between devices  33.4 us (16%)
  starting transfers between devices  18.9 us (9%)
  matrix products  13.7 us (6%)
  other arithmetic  6.39 us (3%)
    unnamed x17, local copies, waits for them, and re-layouts  29.7 us
    all_to_all x2, blocking collectives, moved_by_axis(): lax.all_to_all(pieces, axes[k], split_axis=k, concat_axis=k, tiled=True)  24.7 us
    all_to_all x1, blocking collectives, col_forward(): lax.all_to_all(values, 'col', split_axis=2, concat_axis=3, tiled=True)  22.1 us
    all_to_all x1, blocking collectives, col_backward(): lax.all_to_all(values, 'col', split_axis=3, concat_axis=2, tiled=True)  21.7 us
    all_to_all x1, waiting for transfers between devices, col_forward(): lax.all_to_all(values, 'col', split_axis=2, concat_axis=3, tiled=True)  18.2 us
    all_to_all x1, blocking collectives, on_device(): lax.all_to_all(jnp.stack(jnp.split(spectra[:1], lax.axis_size('col'), axi...  16.5 us
    all_to_all x1, waiting for transfers between devices, row_forward(): return lax.all_to_all(values, ROW, split_axis=2, concat_axis=3, tiled=True)  15.2 us
    all_to_all x4, local copies, waits for them, and re-layouts, col_forward(): lax.all_to_all(values, 'col', split_axis=2, concat_axis=3, tiled=True)  11.3 us
  transfers between devices with their start and end apart: 2, of which 2 were waited for; matrix products, arithmetic and copies ran while one was open for 1% of the time, Pallas kernels for 0%

profile of v1, /device:TPU:128, one launch (start us, length us, event | category | flops | bytes accessed | tf_op | source)
XLA Modules:
  0.0 214.1 jit_solution(3488706897082082830)
XLA Ops:
  0.6 1.0 stack.88
  1.6 1.0 stack.87
  2.6 1.0 subtract_bitcast_fusion
  3.9 0.5 maximum_bitcast_fusion.10
  4.4 1.0 pad_maximum_fusion.1
  5.4 9.7 %all-to-all-start = ((f32[2,2,128,256]{3,1,0,2:T(2,128)}), f32[2,2,128,256]{3,1,0,2:T(2,128)S(1)}, u32[]{:S(2)}, u32[]{:S(2)}) async-start(f32[2,2,128,256]{3,1,0,2:T(2,128)} %pad_maximum_fusion.1), calls=%async_computation | async-start | bytes 1048576 | tf_op jit(solution)/shard_map/all_to_all | solution.py:112
  15.7 18.2 %all-to-all-done = f32[2,2,128,256]{3,1,0,2:T(2,128)S(1)} async-done(((f32[2,2,128,256]{3,1,0,2:T(2,128)}), f32[2,2,128,256]{3,1,0,2:T(2,128)S(1)}, u32[]{:S(2)}, u32[]{:S(2)}) %all-to-all-start) | async-done | bytes 524320 | tf_op jit(solution)/shard_map/all_to_all | solution.py:112
  34.4 1.8 convolution_bitcast_fusion.7
  36.4 1.8 convolution_bitcast_fusion.6
  38.9 8.2 %copy.81 = f32[2,2,4096,8]{3,1,0,2:T(2,128)} copy(f32[2,2,4096,8]{2,3,1,0:T(8,128)S(1)} %bitcast.226) | data formatting | bytes 1048576 | tf_op jit(solution)/shard_map/transpose | solution.py:138
  47.0 14.9 %reshape.452 = f32[16,1,8192]{2,1,0:T(1,128)S(1)} reshape(f32[4096,2,2,8]{3,2,1,0:T(2,128)} %bitcast.224) | data formatting | bytes 1048576
  62.0 22.1 %all_to_all.81 = f32[16,1,8192]{2,1,0:T(1,128)S(1)} all-to-all(f32[16,1,8192]{2,1,0:T(1,128)S(1)} %reshape.452), channel_id=1, replica_groups=mesh['row_0'=8,'row_1'=2,'row_2'=2,'col'=16] {'col'}, dimensions={0} | all-to-all | bytes 1048576 | tf_op jit(solution)/shard_map/all_to_all | solution.py:112
  84.1 0.5 broadcast.663
  84.6 1.9 reduce
  86.5 14.7 %reshape.453 = f32[4096,2,2,8]{3,2,1,0:T(2,128)} reshape(f32[16,8192]{1,0:T(8,128)S(1)} %reduce) | data formatting | bytes 1048576
  101.2 9.5 %copy.82 = f32[2,2,4096,8]{2,3,1,0:T(8,128)S(1)} copy(f32[2,2,4096,8]{3,1,0,2:T(2,128)} %bitcast.225) | data formatting | bytes 1048576 | tf_op jit(solution)/shard_map/all_to_all | solution.py:112
  110.7 1.0 copy.83
  111.7 9.2 %all-to-all-start.2 = ((f32[2,2,256,128]{3,1,0,2:T(2,128)}), f32[2,2,256,128]{3,1,0,2:T(2,128)S(1)}, u32[]{:S(2)}, u32[]{:S(2)}) async-start(f32[2,2,256,128]{3,1,0,2:T(2,128)} %copy.83), calls=%async_computation.2 | async-start | bytes 1048576 | tf_op jit(solution)/shard_map/all_to_all | solution.py:120
  121.5 15.2 %all-to-all-done.2 = f32[2,2,256,128]{3,1,0,2:T(2,128)S(1)} async-done(((f32[2,2,256,128]{3,1,0,2:T(2,128)}), f32[2,2,256,128]{3,1,0,2:T(2,128)S(1)}, u32[]{:S(2)}, u32[]{:S(2)}) %all-to-all-start.2) | async-done | bytes 524320 | tf_op jit(solution)/shard_map/all_to_all | solution.py:120
  137.1 1.8 convolution_bitcast_fusion.5
  139.1 1.8 convolution_bitcast_fusion.4
  141.2 1.0 convolution_bitcast_fusion.3
  142.4 1.8 convolution_bitcast_fusion.2
  144.8 4.2 %all_to_all.82 = f32[16,2,2,2,8,128]{5,0,4,3,2,1:T(8,128)S(1)} all-to-all(f32[16,2,2,2,8,128]{5,0,4,3,2,1:T(8,128)S(1)} %copy.90), channel_id=1, replica_groups=mesh['row_0'=8,'row_1'=2,'row_2'=2,'col'=16] {'row_2'}, dimensions={1} | all-to-all | bytes 1048576 | tf_op jit(solution)/shard_map/all_to_all | solution.py:31
  148.9 0.4 copy.91
  149.3 20.6 %all_to_all.83 = f32[16,2,2,2,8,128]{5,1,4,3,2,0:T(2,128)S(1)} all-to-all(f32[16,2,2,2,8,128]{5,1,4,3,2,0:T(2,128)S(1)} %copy.91), channel_id=1, replica_groups=mesh['row_0'=8,'row_1'=2,'row_2'=2,'col'=16] {'row_0','row_1'}, dimensions={0} | all-to-all | bytes 1048576 | tf_op jit(solution)/shard_map/all_to_all | solution.py:31
  170.3 21.7 %all_to_all.84 = f32[2,2,256,128]{2,1,0,3:T(2,128)S(1)} all-to-all(f32[2,2,256,128]{2,1,0,3:T(2,128)S(1)} %copy.93), channel_id=1, replica_groups=mesh['row_0'=8,'row_1'=2,'row_2'=2,'col'=16] {'col'}, dimensions={3} | all-to-all | bytes 1048576 | tf_op jit(solution)/shard_map/all_to_all | solution.py:116
  192.1 0.4 reshape.431
  192.5 1.8 convolution_bitcast_fusion.1
  194.5 1.8 convolution_bitcast_fusion
  196.9 16.5 %all_to_all.85 = f32[16,1,2,8,256]{4,3,2,1,0:T(8,128)S(1)} all-to-all(f32[16,1,2,8,256]{4,3,2,1,0:T(8,128)S(1)} %constant_dynamic-update-slice_fusion), channel_id=1, replica_groups=mesh['row_0'=8,'row_1'=2,'row_2'=2,'col'=16] {'col'}, dimensions={0} | all-to-all | bytes 524288 | tf_op jit(solution)/shard_map/all_to_all | solution.py:153
  213.4 0.7 slice_bitcast_fusion
  (49 shorter events, 5.3 us)
Async XLA Ops:
  5.4 28.5 %all-to-all-start = ((f32[2,2,128,256]{3,1,0,2:T(2,128)}), f32[2,2,128,256]{3,1,0,2:T(2,128)S(1)}, u32[]{:S(2)}, u32[]{:S(2)}) async-start(f32[2,2,128,256]{3,1,0,2:T(2,128)} %pad_maximum_fusion.1), calls=%async_computation | async-start | bytes 1048576 | tf_op jit(solution)/shard_map/all_to_all | solution.py:112
  111.7 25.0 %all-to-all-start.2 = ((f32[2,2,256,128]{3,1,0,2:T(2,128)}), f32[2,2,256,128]{3,1,0,2:T(2,128)S(1)}, u32[]{:S(2)}, u32[]{:S(2)}) async-start(f32[2,2,256,128]{3,1,0,2:T(2,128)} %copy.83), calls=%async_computation.2 | async-start | bytes 1048576 | tf_op jit(solution)/shard_map/all_to_all | solution.py:120
